TPU v7x, 32 devices: a whole 2x2x4 slice. The times are simulated.
32 devices in a mesh: part: 2 (over x), fsdp: 16 (over z, y, core).
Axes of the slice: x: 2, y: 2, z: 4, core: 2. Of those that a mesh axis runs over, the one named last changes fastest.
Arguments:
- acts_in: bfloat16 [2, 16384, 1024], P(None, ('part', 'fsdp')), parts along dimension 1
- cot_out: bfloat16 [2, 16384, 1024], P(None, ('part', 'fsdp')), parts along dimension 1
- lengths: int32 [2, 32], P(None, ('part', 'fsdp')), parts along dimension 1
- w_up: bfloat16 [2, 1024, 4096], replicated
- w_down: bfloat16 [2, 4096, 1024], replicated
Outputs:
- output 1: float32 [4, 1024, 4096], P('part', 'fsdp'), parts along dimension 0
- output 2: float32 [4, 4096, 1024], P('part', 'fsdp'), parts along dimension 0
There are 2 independent parts. A program takes and returns all parts, laid end to end along the dimension named above; an argument that names none is the same for every part.
All inputs are finite; a program needn't handle non-finite values.
Results may differ from a plain program's by a relative error of at most 0.0097686.
Values are sent between devices in bfloat16 or wider.
A program may use at most 1 GiB of HBM per device.

v0:
```python
import jax
import jax.numpy as jnp
from jax import lax
from jax.sharding import PartitionSpec as P

CONTRACT_LAST = (((1,), (1,)), ((), ()))
CONTRACT_FIRST = (((0,), (0,)), ((), ()))


def gelu_fwd(h_wide):
    return jax.nn.gelu(h_wide, approximate=True)


def gelu_back(h_wide, da_val):
    return jax.vjp(gelu_fwd, h_wide)[1](da_val)[0]


def solution(mesh):
    def local_step(acts_in, cot_out, lengths, w_up, w_down):
        micro, tok_rows, _ = acts_in.shape
        layers = w_up.shape[0]
        keep_mask = (jnp.arange(tok_rows)[None, :] < lengths).astype(jnp.bfloat16)
        acc_up = [None] * layers
        acc_down = [None] * layers
        for k_idx in range(micro):
            x_cur = acts_in[k_idx]
            saved = []
            for layer_idx in range(layers):
                h_val = jnp.dot(x_cur, w_up[layer_idx], preferred_element_type=jnp.float32).astype(jnp.bfloat16)
                a_val = gelu_fwd(h_val.astype(jnp.float32)).astype(jnp.bfloat16)
                y_val = jnp.dot(a_val, w_down[layer_idx], preferred_element_type=jnp.float32).astype(jnp.bfloat16)
                saved.append((x_cur, h_val, a_val))
                x_cur = (x_cur.astype(jnp.float32) + y_val.astype(jnp.float32)).astype(jnp.bfloat16)
            dx_cur = cot_out[k_idx] * keep_mask[k_idx][:, None]
            for layer_idx in reversed(range(layers)):
                x_prev, h_val, a_val = saved[layer_idx]
                da_val = lax.dot_general(dx_cur, w_down[layer_idx], CONTRACT_LAST, preferred_element_type=jnp.float32)
                dh_val = gelu_back(h_val.astype(jnp.float32), da_val).astype(jnp.bfloat16)
                grad_down = lax.dot_general(a_val, dx_cur, CONTRACT_FIRST, preferred_element_type=jnp.float32)
                grad_up = lax.dot_general(x_prev, dh_val, CONTRACT_FIRST, preferred_element_type=jnp.float32)
                if layer_idx > 0:
                    dx_back = lax.dot_general(dh_val, w_up[layer_idx], CONTRACT_LAST, preferred_element_type=jnp.float32)
                    dx_cur = (dx_cur.astype(jnp.float32) + dx_back).astype(jnp.bfloat16)
                shard_down = lax.psum_scatter(grad_down, "fsdp", scatter_dimension=0, tiled=True)
                shard_up = lax.psum_scatter(grad_up, "fsdp", scatter_dimension=0, tiled=True)
                acc_down[layer_idx] = shard_down if acc_down[layer_idx] is None else acc_down[layer_idx] + shard_down
                acc_up[layer_idx] = shard_up if acc_up[layer_idx] is None else acc_up[layer_idx] + shard_up
        return jnp.stack(acc_up), jnp.stack(acc_down)

    act_spec = P(None, ("part", "fsdp"), None)
    grad_spec = P("part", "fsdp", None)
    return jax.shard_map(local_step, mesh=mesh, in_specs=(act_spec, act_spec, P(None, ("part", "fsdp")), P(), P()), out_specs=(grad_spec, grad_spec), check_vma=False)
```

profile of v0, /device:TPU:0, one launch (start us, length us, event | category | flops | bytes accessed | tf_op | source)
XLA Modules:
  0.0 839.3 jit_solution(2063910304425102131)
XLA Ops:
  7.2 10.3 %fusion.68 = bf16[512,4096]{1,0:T(8,128)(2,1)} fusion(bf16[2,1024,4096]{2,1,0:T(8,128)(2,1)} %param.8, bf16[2,512,1024]{2,1,0:T(8,128)(2,1)} %param.5), kind=kOutput, calls=%fused_computation.90 | convolution fusion | flops 4297064448 | bytes 13631488 | tf_op jit(solution)/shard_map/dot_general | solution.py:29
  17.6 5.1 fusion.71
  22.8 11.4 %add_convert_fusion.3 = bf16[512,1024]{1,0:T(8,128)(2,1)S(1)} fusion(bf16[2,4096,1024]{2,1,0:T(8,128)(2,1)} %param.9, bf16[2,512,1024]{2,1,0:T(8,128)(2,1)S(1)} %copy-done.5, bf16[512,4096]{1,0:T(8,128)(2,1)} %fusion.68), kind=kOutput, calls=%fused_computation.124 | convolution fusion | flops 4318560256 | bytes 14680064 | tf_op jit(solution)/shard_map/dot_general | solution.py:31
  34.3 8.8 %add_convert_fusion.1 = bf16[512,1024]{1,0:T(8,128)(2,1)S(1)} fusion(bf16[2,4096,1024]{2,1,0:T(8,128)(2,1)} %param.9, bf16[2,512,1024]{2,1,0:T(8,128)(2,1)S(1)} %copy-done.5, bf16[512,4096]{1,0:T(8,128)(2,1)S(1)} %fusion.71), kind=kOutput, calls=%fused_computation.122 | convolution fusion | flops 4318560256 | bytes 14680064 | tf_op jit(solution)/shard_map/dot_general | solution.py:31
  43.1 8.7 %fusion.77 = bf16[512,4096]{1,0:T(8,128)(2,1)S(1)} fusion(bf16[512,1024]{1,0:T(8,128)(2,1)S(1)} %add_convert_fusion.1, bf16[2,1024,4096]{2,1,0:T(8,128)(2,1)} %param.8), kind=kOutput, calls=%fused_computation.93 | convolution fusion | flops 4297064448 | bytes 13631488 | tf_op jit(solution)/shard_map/dot_general | solution.py:29
  51.8 9.6 %fusion.74 = bf16[512,4096]{1,0:T(8,128)(2,1)S(1)} fusion(bf16[512,1024]{1,0:T(8,128)(2,1)S(1)} %add_convert_fusion.3, bf16[2,1024,4096]{2,1,0:T(8,128)(2,1)} %param.8), kind=kOutput, calls=%fused_computation.92 | convolution fusion | flops 4297064448 | bytes 13631488 | tf_op jit(solution)/shard_map/dot_general | solution.py:29
  61.4 12.9 %fusion.12 = bf16[512,4096]{1,0:T(8,128)(2,1)S(1)} fusion(bf16[512,4096]{1,0:T(8,128)(2,1)S(1)} %fusion.74, bf16[2,4096,1024]{2,1,0:T(8,128)(2,1)} %param.9, bf16[2,512,1024]{2,1,0:T(8,128)(2,1)S(1)} %copy-done.6, bf16[512]{0:T(512)(128)(2,1)S(1)} %get-tuple-element.7), kind=kOutput, calls=%fused_computation.33 | convolution fusion | flops 4339531776 | bytes 17826816 | tf_op jit(solution)/shard_map/dot_general | solution.py:37
  74.4 8.1 fusion.182
  82.5 11.6 %fusion.6 = bf16[512,4096]{1,0:T(8,128)(2,1)S(1)} fusion(bf16[512,4096]{1,0:T(8,128)(2,1)S(1)} %fusion.77, bf16[2,4096,1024]{2,1,0:T(8,128)(2,1)} %param.9, bf16[2,512,1024]{2,1,0:T(8,128)(2,1)S(1)} %copy-done.6, bf16[512]{0:T(512)(128)(2,1)S(1)} %get-tuple-element.6), kind=kOutput, calls=%fused_computation.27 | convolution fusion | flops 4339531776 | bytes 17826816 | tf_op jit(solution)/shard_map/dot_general | solution.py:37
  94.1 1.9 copy-done
  96.1 11.6 %convolution_add_fusion = f32[1024,4096]{1,0:T(8,128)} fusion(f32[1024,4096]{1,0:T(8,128)} %fusion.182, bf16[512,1024]{1,0:T(8,128)(2,1)S(1)} %add_convert_fusion.1, bf16[512,4096]{1,0:T(8,128)(2,1)S(1)} %fusion.6), kind=kOutput, calls=%fused_computation.85 | convolution fusion | flops 4299161600 | bytes 38797312 | tf_op jit(solution)/shard_map/dot_general | solution.py:40
  107.9 9.5 %add_convert_fusion = bf16[512,1024]{1,0:T(8,128)(2,1)S(1)} fusion(bf16[512,4096]{1,0:T(8,128)(2,1)} %copy-done, bf16[2,1024,4096]{2,1,0:T(8,128)(2,1)} %param.8, bf16[2,512,1024]{2,1,0:T(8,128)(2,1)} %param.6, bf16[512]{0:T(512)(128)(2,1)S(1)} %get-tuple-element.6), kind=kOutput, calls=%fused_computation.121 | convolution fusion | flops 4297064448 | bytes 14681088 | tf_op jit(solution)/shard_map/dot_general | solution.py:42
  117.4 10.5 %add_convert_fusion.2 = bf16[512,1024]{1,0:T(8,128)(2,1)} fusion(bf16[512,4096]{1,0:T(8,128)(2,1)S(1)} %copy-done.2, bf16[2,1024,4096]{2,1,0:T(8,128)(2,1)} %param.8, bf16[2,512,1024]{2,1,0:T(8,128)(2,1)S(1)} %copy-done.7, bf16[512]{0:T(512)(128)(2,1)S(1)} %get-tuple-element.7), kind=kOutput, calls=%fused_computation.123 | convolution fusion | flops 4297064448 | bytes 14681088 | tf_op jit(solution)/shard_map/dot_general | solution.py:42
  127.9 20.6 %fusion.109 = f32[4096,1024]{1,0:T(8,128)} fusion(bf16[512,4096]{1,0:T(8,128)(2,1)} %fusion.68, bf16[512,1024]{1,0:T(8,128)(2,1)} %add_convert_fusion.2, bf16[2,4096,1024]{2,1,0:T(8,128)(2,1)} %param.9, bf16[2,512,1024]{2,1,0:T(8,128)(2,1)S(1)} %copy-done.5), kind=kOutput, calls=%fused_computation.119 | convolution fusion | flops 8633974784 | bytes 31457280 | tf_op jit(solution)/shard_map/dot_general | solution.py:40
  148.5 21.1 %add_bitcast_fusion = f32[1024,4096]{0,1:T(8,128)} fusion(f32[4096,1024]{1,0:T(8,128)} %fusion.109, bf16[512,4096]{1,0:T(8,128)(2,1)} %copy-done.9, bf16[512,1024]{1,0:T(8,128)(2,1)S(1)} %add_convert_fusion, bf16[2,4096,1024]{2,1,0:T(8,128)(2,1)} %param.9, bf16[2,512,1024]{2,1,0:T(8,128)(2,1)S(1)} %copy-done.5), kind=kOutput, calls=%fused_computation | convolution fusion | flops 8638169088 | bytes 48234496 | tf_op jit(solution)/shard_map/dot_general | solution.py:40
  169.6 17.5 %copy.12 = f32[1024,4096]{1,0:T(8,128)} copy(f32[1024,4096]{0,1:T(8,128)} %add_bitcast_fusion) | data formatting | bytes 33554432
  187.1 0.6 reduce-scatter.11.cloned.1.call-start
  187.7 1.0 copy-done.8
  188.7 14.5 %fusion.89 = f32[4096,1024]{1,0:T(8,128)} fusion(bf16[512,4096]{1,0:T(8,128)(2,1)} %copy-done.13, bf16[2,512,1024]{2,1,0:T(8,128)(2,1)S(1)} %copy-done.8, bf16[512]{0:T(512)(128)(2,1)S(1)} %get-tuple-element.7), kind=kOutput, calls=%fused_computation.104 | convolution fusion | flops 4316463104 | bytes 22021120 | tf_op jit(solution)/shard_map/dot_general | solution.py:39
  203.2 13.5 %convolution_add_fusion.1 = f32[4096,1024]{1,0:T(8,128)} fusion(f32[4096,1024]{1,0:T(8,128)} %fusion.89, bf16[512,4096]{1,0:T(8,128)(2,1)S(1)} %copy-done.12, bf16[2,512,1024]{2,1,0:T(8,128)(2,1)S(1)} %copy-done.8, bf16[512]{0:T(512)(128)(2,1)S(1)} %get-tuple-element.6), kind=kOutput, calls=%fused_computation.94 | convolution fusion | flops 4320657408 | bytes 38798336 | tf_op jit(solution)/shard_map/dot_general | solution.py:39
  217.0 1.0 copy-done.14
  218.0 14.0 %fusion.179 = f32[4096,1024]{1,0:T(8,128)} fusion(bf16[512,1024]{1,0:T(8,128)(2,1)S(1)} %copy-done.14, bf16[512,4096]{1,0:T(8,128)(2,1)} %fusion.68), kind=kOutput, calls=%fused_computation.172 | convolution fusion | flops 4315938816 | bytes 22020096 | tf_op jit(solution)/shard_map/dot_general | solution.py:39
  232.0 13.4 %convolution_add_fusion.2 = f32[4096,1024]{1,0:T(8,128)} fusion(f32[4096,1024]{1,0:T(8,128)} %fusion.179, bf16[512,1024]{1,0:T(8,128)(2,1)S(1)} %add_convert_fusion, bf16[512,4096]{1,0:T(8,128)(2,1)S(1)} %copy-done.10), kind=kOutput, calls=%fused_computation.95 | convolution fusion | flops 4320133120 | bytes 38797312 | tf_op jit(solution)/shard_map/dot_general | solution.py:39
  245.5 42.4 %reduce-scatter.15.cloned.1.call-done = f32[64,4096]{1,0:T(8,128)} async-done(((f32[1024,4096]{1,0:T(8,128)}), f32[64,4096]{1,0:T(8,128)}) %reduce-scatter.15.cloned.1.call-update) | async-done | bytes 1048592
  287.8 1.8 copy.15
  289.7 178.8 %reduce-scatter.13.cloned.1.call-done = f32[64,4096]{1,0:T(8,128)} async-done(((f32[1024,4096]{1,0:T(8,128)}), f32[64,4096]{1,0:T(8,128)}) %reduce-scatter.13.cloned.1.call-update) | async-done | bytes 1048592
  468.4 3.2 copy.13
  471.6 3.8 pad_maximum_fusion
  475.4 4.3 copy.11
  479.7 169.3 %reduce-scatter.11.cloned.1.call-done = f32[256,1024]{1,0:T(8,128)} async-done(((f32[4096,1024]{1,0:T(8,128)}), f32[256,1024]{1,0:T(8,128)}) %reduce-scatter.11.cloned.1.call-update) | async-done | bytes 1048592 | tf_op jit(solution)/shard_map/reduce_scatter | solution.py:44
  649.0 180.4 %reduce-scatter.9.cloned.1.call-done = f32[256,1024]{1,0:T(8,128)} async-done(((f32[4096,1024]{1,0:T(8,128)}), f32[256,1024]{1,0:T(8,128)}) %reduce-scatter.9.cloned.1.call-update) | async-done | bytes 1048592 | tf_op jit(solution)/shard_map/reduce_scatter | solution.py:44
  829.4 3.1 pad_maximum_fusion.1
  (36 shorter events, 0.7 us)
Async XLA Ops:
  7.2 10.4 %copy-start.5 = (bf16[2,512,1024]{2,1,0:T(8,128)(2,1)S(1)}, bf16[2,512,1024]{2,1,0:T(8,128)(2,1)}, u32[]{:S(2)}) copy-start(bf16[2,512,1024]{2,1,0:T(8,128)(2,1)} %param.5) | copy-start | bytes 6291460
  7.2 280.7 %reduce-scatter.15.cloned.1.call-start = ((), (), s32[]{:S(2)}) async-start(), calls=%async_computation.7 | async-start | bytes 17825792
  7.2 10.4 %copy-start.4 = (bf16[2,1024,4096]{2,1,0:T(8,128)(2,1)S(1)}, bf16[2,1024,4096]{2,1,0:T(8,128)(2,1)}, u32[]{:S(2)}) copy-start(bf16[2,1024,4096]{2,1,0:T(8,128)(2,1)} %param.8) | copy-start | bytes 50331652
  17.6 5.1 copy-start.3
  22.7 11.6 %copy-start.9 = (bf16[512,4096]{1,0:T(8,128)(2,1)}, bf16[512,4096]{1,0:T(8,128)(2,1)S(1)}, u32[]{:S(2)}) copy-start(bf16[512,4096]{1,0:T(8,128)(2,1)S(1)} %fusion.71) | copy-start | bytes 12582916
  51.7 30.8 %copy-start.11 = (bf16[512,4096]{1,0:T(8,128)(2,1)}, bf16[512,4096]{1,0:T(8,128)(2,1)S(1)}, u32[]{:S(2)}) copy-start(bf16[512,4096]{1,0:T(8,128)(2,1)S(1)} %fusion.77) | copy-start | bytes 12582916
  51.8 9.7 %copy-start.6 = (bf16[2,512,1024]{2,1,0:T(8,128)(2,1)S(1)}, bf16[2,512,1024]{2,1,0:T(8,128)(2,1)}, u32[]{:S(2)}) copy-start(bf16[2,512,1024]{2,1,0:T(8,128)(2,1)} %param.6) | copy-start | bytes 6291460
  61.4 13.0 %copy-start.13 = (bf16[512,4096]{1,0:T(8,128)(2,1)}, bf16[512,4096]{1,0:T(8,128)(2,1)S(1)}, u32[]{:S(2)}) copy-start(bf16[512,4096]{1,0:T(8,128)(2,1)S(1)} %fusion.74) | copy-start | bytes 12582916
  74.4 8.2 copy-start.1
  94.1 1.9 copy-start
  107.6 360.8 %reduce-scatter.13.cloned.1.call-start = ((), (), s32[]{:S(2)}) async-start(), calls=%async_computation.6 | async-start | bytes 17825792
  107.9 9.5 %copy-start.2 = (bf16[512,4096]{1,0:T(8,128)(2,1)S(1)}, bf16[512,4096]{1,0:T(8,128)(2,1)}, u32[]{:S(2)}) copy-start(bf16[512,4096]{1,0:T(8,128)(2,1)} %copy-done.1) | copy-start | bytes 12582916
  107.9 9.5 %copy-start.7 = (bf16[2,512,1024]{2,1,0:T(8,128)(2,1)S(1)}, bf16[2,512,1024]{2,1,0:T(8,128)(2,1)}, u32[]{:S(2)}) copy-start(bf16[2,512,1024]{2,1,0:T(8,128)(2,1)} %param.6) | copy-start | bytes 6291460
  187.1 1.6 copy-start.8
  187.1 461.8 %reduce-scatter.11.cloned.1.call-start = ((), (), s32[]{:S(2)}) async-start(), calls=%async_computation.5 | async-start | bytes 17825792 | tf_op jit(solution)/shard_map/reduce_scatter | solution.py:44
  188.7 14.5 %copy-start.12 = (bf16[512,4096]{1,0:T(8,128)(2,1)S(1)}, bf16[512,4096]{1,0:T(8,128)(2,1)}, u32[]{:S(2)}) copy-start(bf16[512,4096]{1,0:T(8,128)(2,1)} %copy-done.11) | copy-start | bytes 12582916
  216.7 1.3 copy-start.14
  216.8 612.7 %reduce-scatter.9.cloned.1.call-start = ((), (), s32[]{:S(2)}) async-start(), calls=%async_computation.4 | async-start | bytes 17825792 | tf_op jit(solution)/shard_map/reduce_scatter | solution.py:44
  218.0 14.0 %copy-start.10 = (bf16[512,4096]{1,0:T(8,128)(2,1)S(1)}, bf16[512,4096]{1,0:T(8,128)(2,1)}, u32[]{:S(2)}) copy-start(bf16[512,4096]{1,0:T(8,128)(2,1)} %copy-done.9) | copy-start | bytes 12582916
Sparse Core Ops, SparseCore 0:
  107.8 180.0 reduce-scatter.14
  291.9 176.4 reduce-scatter.12
  472.5 176.4 reduce-scatter.10
  653.0 176.4 reduce-scatter.8
where the time goes:
time: 843 us; the launch traced here: 839 us
  waiting for transfers between devices  571 us (68%)
  matrix products  215 us (26%)
  local copies, waits for them, and re-layouts  30.8 us (4%)
  between operations  14.2 us (2%)
    reduce_scatter x2, waiting for transfers between devices, local_step(): lax.psum_scatter(grad_down, 'fsdp', scatter_dimension=0, tiled=True)  350 us
    unnamed x6, waiting for transfers between devices  221 us
    dot_general x4, matrix products, local_step(): lax.dot_general(x_prev, dh_val, CONTRACT_FIRST, preferred_element_type=jn...  61.4 us
    dot_general x4, matrix products, local_step(): lax.dot_general(a_val, dx_cur, CONTRACT_FIRST, preferred_element_type=jnp...  55.5 us
    dot_general x4, matrix products, local_step(): jnp.dot(x_cur, w_up[layer_idx], preferred_element_type=jnp.float32)  33.7 us
    unnamed x34, local copies, waits for them, and re-layouts  30.8 us
    dot_general x2, matrix products, local_step(): lax.dot_general(dx_cur, w_down[layer_idx], CONTRACT_LAST, preferred_eleme...  24.5 us
    dot_general x2, matrix products, local_step(): jnp.dot(a_val, w_down[layer_idx], preferred_element_type=jnp.float32)  20.2 us
  transfers between devices with their start and end apart: 4, of which 4 were waited for; matrix products, arithmetic and copies ran while one was open for 18% of the time, Pallas kernels for 0%

commit v1 on v0

v1 whole, which is shorter than its diff:
```python
import jax
import jax.numpy as jnp
from jax import lax
from jax.sharding import Mesh, PartitionSpec as P


CONTRACT_LAST = (((1,), (1,)), ((), ()))
CONTRACT_FIRST = (((0,), (0,)), ((), ()))


def gelu_fwd(h_wide):
    return jax.nn.gelu(h_wide, approximate=True)


def gelu_back(h_wide, da_val):
    return jax.vjp(gelu_fwd, h_wide)[1](da_val)[0]


def dot_f32(lhs, rhs, dims=(((1,), (0,)), ((), ()))):
    return lax.dot_general(lhs, rhs, dims, preferred_element_type=jnp.float32)


SWAP = [(0, 1), (1, 0)]


def gather_quad(tok):
    other = lax.ppermute(tok, "y", SWAP)
    pair = jnp.concatenate([tok, other], axis=0)
    other = lax.ppermute(pair, "core", SWAP)
    return jnp.concatenate([pair, other], axis=0)


def solution(mesh):
    quad = 4
    n_z = mesh.shape["fsdp"] // quad
    fine = Mesh(mesh.devices.reshape(mesh.shape["part"], n_z, 2, 2), ("part", "z", "y", "core"))
    fsdp = ("z", "y", "core")

    def local_step(acts_in, cot_out, lengths, w_up, w_down):
        micro, tok_rows, width = acts_in.shape
        hidden = w_up.shape[2]
        own = hidden // (n_z * quad)
        q_idx = lax.axis_index("y") * 2 + lax.axis_index("core")
        keep = jnp.arange(tok_rows)[None, :] < lengths
        r_val = jnp.where(keep[:, :, None], cot_out, jnp.zeros_like(cot_out)).reshape(micro * tok_rows, width)
        x_0 = acts_in.reshape(micro * tok_rows, width)

        dx_2_all = gather_quad(r_val)

        h_val = dot_f32(x_0, w_up[0]).astype(jnp.bfloat16)
        a_val = gelu_fwd(h_val.astype(jnp.float32)).astype(jnp.bfloat16)
        y_val = dot_f32(a_val, w_down[0]).astype(jnp.bfloat16)
        x_1 = (x_0.astype(jnp.float32) + y_val.astype(jnp.float32)).astype(jnp.bfloat16)
        x_1_all = gather_quad(x_1)
        x_0_all = gather_quad(x_0)
        h_val = dot_f32(x_1, w_up[1]).astype(jnp.bfloat16)
        da_val = dot_f32(r_val, w_down[1], CONTRACT_LAST)
        dh_val = gelu_back(h_val.astype(jnp.float32), da_val).astype(jnp.bfloat16)
        dx_back = dot_f32(dh_val, w_up[1], CONTRACT_LAST)
        dx_1 = (r_val.astype(jnp.float32) + dx_back).astype(jnp.bfloat16)
        dx_1_all = gather_quad(dx_1)

        def slice_grads(layer, x_all, dx_all):
            cols = [z_idx * quad * own + q_idx * own for z_idx in range(n_z)]
            w_in = [lax.dynamic_slice(w_up, (layer, 0, col), (1, width, own))[0] for col in cols]
            w_in = jnp.concatenate(w_in, axis=1)
            w_out = [lax.dynamic_slice(w_down, (layer, col, 0), (1, own, width))[0] for col in cols]
            w_out = jnp.concatenate(w_out, axis=0)
            h_sl = dot_f32(x_all, w_in).astype(jnp.bfloat16)
            h_wide = h_sl.astype(jnp.float32)
            a_sl = gelu_fwd(h_wide).astype(jnp.bfloat16)
            da_sl = dot_f32(dx_all, w_out, CONTRACT_LAST)
            dh_sl = gelu_back(h_wide, da_sl).astype(jnp.bfloat16)
            part_up = dot_f32(x_all, dh_sl, CONTRACT_FIRST)
            sum_up = lax.psum_scatter(part_up, "z", scatter_dimension=0, tiled=True)
            part_down = dot_f32(a_sl, dx_all, CONTRACT_FIRST)
            sum_down = lax.psum_scatter(part_down, "z", scatter_dimension=0, tiled=True)
            rows = width // (n_z * quad)
            swapped = lax.all_to_all(sum_up.reshape(quad, rows, n_z * own), ("y", "core"), 0, 0)
            full = swapped.reshape(quad, rows, n_z, own).transpose(1, 2, 0, 3).reshape(rows, hidden)
            return full, sum_down

        up_1, down_1 = slice_grads(1, x_1_all, dx_2_all)
        up_0, down_0 = slice_grads(0, x_0_all, dx_1_all)
        return jnp.stack([up_0, up_1]), jnp.stack([down_0, down_1])

    act_spec = P(None, ("part",) + fsdp, None)
    grad_spec = P("part", fsdp, None)
    return jax.shard_map(
        local_step,
        mesh=fine,
        in_specs=(act_spec, act_spec, P(None, ("part",) + fsdp), P(), P()),
        out_specs=(grad_spec, grad_spec),
        check_vma=False,
    )
```

time: 843 us -> 593 us (0.70)
  waiting for transfers between devices: 571 us -> 286 us
  matrix products: 215 us -> 234 us
  local copies, waits for them, and re-layouts: 30.8 us -> 12 us
  other arithmetic: 6.99 us -> 23 us
  starting transfers between devices: 1.07 us -> 15.8 us
    unnamed x6 -> x4, waiting for transfers between devices: 221 us -> 0.07 us
    reduce_scatter x2 -> x4, waiting for transfers between devices: 350 us -> 213 us  [the longest x2 155 us: slice_grads(): sum_down = lax.psum_scatter(part_down, 'z', scatter_dimension=0, tiled=True)]
    ppermute x0 -> x8, waiting for transfers between devices: none -> 72.9 us  [the longest x4 72.9 us: gather_quad(): other = lax.ppermute(tok, 'y', SWAP)]
    unnamed x34 -> x8, local copies, waits for them, and re-layouts: 30.8 us -> 0.02 us
    dot_general x18 -> x12, matrix products: 215 us -> 234 us  [dot_f32(): return lax.dot_general(lhs, rhs, dims, preferred_element_type=jnp.float32)]
    concatenate x0 -> x4, other arithmetic: none -> 16.6 us  [gather_quad(): pair = jnp.concatenate([tok, other], axis=0)]
    squeeze x0 -> x2, local copies, waits for them, and re-layouts: none -> 8.57 us  [the longest x1 4.39 us: slice_grads(): lax.dynamic_slice(w_up, (layer, 0, col), (1, width, own))[0]]
  transfers between devices with their start and end apart: 4 -> 14, of which waited for: 4 -> 6; matrix products, arithmetic and copies ran while one was open for 18% -> 45% of each run, Pallas kernels for 0% -> 0%
where the time goes in v1:
time: 593 us; the launch traced here: 585 us
  waiting for transfers between devices  286 us (48%)
  matrix products  234 us (39%)
  other arithmetic  23 us (4%)
  starting transfers between devices  15.8 us (3%)
  between operations  14.3 us (2%)
  local copies, waits for them, and re-layouts  12 us (2%)
    dot_general x12, matrix products, dot_f32(): return lax.dot_general(lhs, rhs, dims, preferred_element_type=jnp.float32)  234 us
    reduce_scatter x2, waiting for transfers between devices, slice_grads(): sum_down = lax.psum_scatter(part_down, 'z', scatter_dimension=0, tiled=True)  155 us
    ppermute x4, waiting for transfers between devices, gather_quad(): other = lax.ppermute(tok, 'y', SWAP)  72.9 us
    reduce_scatter x2, waiting for transfers between devices, slice_grads(): sum_up = lax.psum_scatter(part_up, 'z', scatter_dimension=0, tiled=True)  57.7 us
    concatenate x4, other arithmetic, gather_quad(): pair = jnp.concatenate([tok, other], axis=0)  16.6 us
  transfers between devices with their start and end apart: 14, of which 6 were waited for; matrix products, arithmetic and copies ran while one was open for 45% of the time, Pallas kernels for 0%

profile of v1, /device:TPU:0, one launch (start us, length us, event | category | flops | bytes accessed | tf_op | source)
XLA Modules:
  0.0 584.9 jit_solution(9352891614159492476)
XLA Ops:
  7.2 3.1 collective-permute-start
  10.3 25.3 %add_convert_fusion.1 = bf16[1024,1024]{1,0:T(8,128)(2,1)} fusion(bf16[1024,1024]{1,0:T(8,128)(2,1)} %bitcast.83, bf16[2,4096,1024]{2,1,0:T(8,128)(2,1)} %param.9, bf16[2,1024,4096]{2,1,0:T(8,128)(2,1)} %param.8), kind=kOutput, calls=%fused_computation.87 | convolution fusion | flops 17231249408 | bytes 23068672 | tf_op jit(solution)/shard_map/dot_general | solution.py:20
  35.7 1.8 broadcast_select_fusion
  37.5 2.1 collective-permute-start.6
  39.6 14.7 %fusion.37 = bf16[1024,4096]{1,0:T(8,128)(2,1)} fusion(bf16[1024,1024]{1,0:T(8,128)(2,1)} %add_convert_fusion.1, bf16[2,1024,4096]{2,1,0:T(8,128)(2,1)} %param.8), kind=kOutput, calls=%fused_computation.59 | convolution fusion | flops 8589934592 | bytes 18874368 | tf_op jit(solution)/shard_map/dot_general | solution.py:20
  54.3 14.8 %fusion.43 = f32[1024,4096]{1,0:T(8,128)} fusion(bf16[1024,1024]{1,0:T(8,128)(2,1)S(1)} %bitcast.75, bf16[2,4096,1024]{2,1,0:T(8,128)(2,1)} %param.9), kind=kOutput, calls=%fused_computation.65 | convolution fusion | flops 8589934592 | bytes 27262976 | tf_op jit(solution)/shard_map/dot_general | solution.py:20
  69.1 33.0 %collective-permute-done.4 = bf16[1024,1024]{1,0:T(8,128)(2,1)} collective-permute-done((bf16[1024,1024]{1,0:T(8,128)(2,1)}, bf16[1024,1024]{1,0:T(8,128)(2,1)}, u32[]{:S(2)}, u32[]{:S(2)}) %collective-permute-start.4) | collective-permute-done | bytes 2097184 | tf_op jit(solution)/shard_map/ppermute | solution.py:27
  102.0 4.6 pad_maximum_fusion.6
  106.6 25.3 %add_convert_fusion = bf16[1024,1024]{1,0:T(8,128)(2,1)} fusion(bf16[1024,1024]{1,0:T(8,128)(2,1)S(1)} %bitcast.76, bf16[2,1024,4096]{2,1,0:T(8,128)(2,1)} %param.8, f32[1024,4096]{1,0:T(8,128)} %fusion.43, bf16[1024,4096]{1,0:T(8,128)(2,1)} %fusion.37), kind=kOutput, calls=%fused_computation.86 | convolution fusion | flops 8681160704 | bytes 37748736 | tf_op jit(solution)/shard_map/dot_general | solution.py:20
  132.0 2.1 collective-permute-start.2
  134.0 12.9 %collective-permute-done.6 = bf16[1024,1024]{1,0:T(8,128)(2,1)} collective-permute-done((bf16[1024,1024]{1,0:T(8,128)(2,1)S(1)}, bf16[1024,1024]{1,0:T(8,128)(2,1)}, u32[]{:S(2)}, u32[]{:S(2)}) %collective-permute-start.6) | collective-permute-done | bytes 2097184 | tf_op jit(solution)/shard_map/ppermute | solution.py:27
  147.0 4.0 pad_maximum_fusion.7
  151.0 4.2 dynamic-slice_bitcast_fusion.15
  155.1 4.4 dynamic-slice_bitcast_fusion.11
  159.5 4.0 pad_maximum_fusion.4
  164.1 27.0 %collective-permute-done.2 = bf16[1024,1024]{1,0:T(8,128)(2,1)} collective-permute-done((bf16[1024,1024]{1,0:T(8,128)(2,1)}, bf16[1024,1024]{1,0:T(8,128)(2,1)}, u32[]{:S(2)}, u32[]{:S(2)}) %collective-permute-start.2) | collective-permute-done | bytes 2097184 | tf_op jit(solution)/shard_map/ppermute | solution.py:27
  191.1 4.0 pad_maximum_fusion.5
  195.0 16.1 %convolution_convert_fusion = bf16[4096,1024]{1,0:T(8,128)(2,1)} fusion(bf16[2048,1024]{1,0:T(8,128)(2,1)} %collective-permute-done.5, bf16[1024,1024]{1,0:T(8,128)(2,1)} %collective-permute-done.4, bf16[1024,1024]{1,0:T(8,128)(2,1)} %add_convert_fusion.1, bf16[1024,256]{1,0:T(8,128)(2,1)} %get-tuple-element.16, bf16[1024,256]{1,0:T(8,128)(2,1)} %get-tuple-element.17, ...), kind=kOutput, calls=%fused_computation.78 | convolution fusion | flops 8627683328 | bytes 18874368 | tf_op jit(solution)/shard_map/dot_general | solution.py:20
  211.1 26.4 %fusion.173 = bf16[4096,1024]{1,0:T(8,128)(2,1)} fusion(bf16[4096,1024]{1,0:T(8,128)(2,1)} %convolution_convert_fusion, bf16[2048,1024]{1,0:T(8,128)(2,1)} %collective-permute-done.7, bf16[1024,1024]{1,0:T(8,128)(2,1)} %collective-permute-done.6, bf16[1024,1024]{1,0:T(8,128)(2,1)S(1)} %bitcast.78, bf16[256,1024]{1,0:T(8,128)(2,1)} %get-tuple-element.8, ...), kind=kOutput, calls=%fused_computation.23.clone.clone | convolution fusion | flops 8711569408 | bytes 27262976 | tf_op jit(solution)/shard_map/dot_general | solution.py:20
  237.5 15.0 %fusion.60 = f32[1024,1024]{1,0:T(8,128)} fusion(bf16[2048,1024]{1,0:T(8,128)(2,1)} %collective-permute-done.5, bf16[1024,1024]{1,0:T(8,128)(2,1)} %collective-permute-done.4, bf16[1024,1024]{1,0:T(8,128)(2,1)} %add_convert_fusion.1, bf16[4096,1024]{1,0:T(8,128)(2,1)} %fusion.173), kind=kOutput, calls=%fused_computation.77 | convolution fusion | flops 8615100416 | bytes 20971520 | tf_op jit(solution)/shard_map/dot_general | solution.py:20
  252.8 16.1 %convolution_convert_fusion.1 = bf16[4096,1024]{1,0:T(8,128)(2,1)} fusion(bf16[2048,1024]{1,0:T(8,128)(2,1)} %collective-permute-done.1, bf16[1024,1024]{1,0:T(8,128)(2,1)} %collective-permute-done, bf16[1024,1024]{1,0:T(8,128)(2,1)} %bitcast.84, bf16[1024,256]{1,0:T(8,128)(2,1)} %get-tuple-element.13, bf16[1024,256]{1,0:T(8,128)(2,1)} %get-tuple-element.14, ...), kind=kOutput, calls=%fused_computation.79 | convolution fusion | flops 8627683328 | bytes 18874368 | tf_op jit(solution)/shard_map/dot_general | solution.py:20
  268.9 26.4 %fusion.170 = bf16[4096,1024]{1,0:T(8,128)(2,1)} fusion(bf16[4096,1024]{1,0:T(8,128)(2,1)} %convolution_convert_fusion.1, bf16[2048,1024]{1,0:T(8,128)(2,1)} %collective-permute-done.3, bf16[1024,1024]{1,0:T(8,128)(2,1)} %collective-permute-done.2, bf16[1024,1024]{1,0:T(8,128)(2,1)} %add_convert_fusion, ...), kind=kOutput, calls=%fused_computation.26.clone.clone.2 | convolution fusion | flops 8711569408 | bytes 27262976 | tf_op jit(solution)/shard_map/dot_general | solution.py:20
  295.4 14.9 %fusion.58 = f32[1024,1024]{1,0:T(8,128)} fusion(bf16[2048,1024]{1,0:T(8,128)(2,1)} %collective-permute-done.1, bf16[1024,1024]{1,0:T(8,128)(2,1)} %collective-permute-done, bf16[1024,1024]{1,0:T(8,128)(2,1)S(1)} %bitcast.86, bf16[4096,1024]{1,0:T(8,128)(2,1)} %fusion.170), kind=kOutput, calls=%fused_computation.76 | convolution fusion | flops 8615100416 | bytes 20971520 | tf_op jit(solution)/shard_map/dot_general | solution.py:20
  310.5 19.1 %fusion.53 = f32[1024,1024]{1,0:T(8,128)} fusion(bf16[4096,1024]{1,0:T(8,128)(2,1)} %convolution_convert_fusion, bf16[2048,1024]{1,0:T(8,128)(2,1)} %collective-permute-done.7, bf16[1024,1024]{1,0:T(8,128)(2,1)} %collective-permute-done.6, bf16[1024,1024]{1,0:T(8,128)(2,1)S(1)} %bitcast.79), kind=kOutput, calls=%fused_computation.74 | convolution fusion | flops 8657043456 | bytes 20971520 | tf_op jit(solution)/shard_map/dot_general | solution.py:20
  329.8 19.7 %fusion.55 = f32[1024,1024]{1,0:T(8,128)} fusion(bf16[4096,1024]{1,0:T(8,128)(2,1)} %convolution_convert_fusion.1, bf16[2048,1024]{1,0:T(8,128)(2,1)} %collective-permute-done.3, bf16[1024,1024]{1,0:T(8,128)(2,1)} %collective-permute-done.2, bf16[1024,1024]{1,0:T(8,128)(2,1)} %add_convert_fusion), kind=kOutput, calls=%fused_computation.75 | convolution fusion | flops 8657043456 | bytes 20971520 | tf_op jit(solution)/shard_map/dot_general | solution.py:20
  349.6 3.5 all-to-all-start.1
  353.1 57.7 %reduce-scatter.5.cloned.1.call-done = f32[256,1024]{1,0:T(8,128)} async-done(((f32[1024,1024]{1,0:T(8,128)}), f32[256,1024]{1,0:T(8,128)}) %reduce-scatter.5.cloned.1.call-update) | async-done | bytes 1048592 | tf_op jit(solution)/shard_map/reduce_scatter | solution.py:75
  410.8 3.8 all-to-all-start
  414.5 75.9 %reduce-scatter.11.cloned.1.call-done = f32[256,1024]{1,0:T(8,128)} async-done(((f32[1024,1024]{1,0:T(8,128)}), f32[256,1024]{1,0:T(8,128)}) %reduce-scatter.11.cloned.1.call-update) | async-done | bytes 1048592 | tf_op jit(solution)/shard_map/reduce_scatter | solution.py:77
  490.4 79.5 %reduce-scatter.9.cloned.1.call-done = f32[256,1024]{1,0:T(8,128)} async-done(((f32[1024,1024]{1,0:T(8,128)}), f32[256,1024]{1,0:T(8,128)}) %reduce-scatter.9.cloned.1.call-update) | async-done | bytes 1048592 | tf_op jit(solution)/shard_map/reduce_scatter | solution.py:77
  569.9 3.1 pad_maximum_fusion.25
  576.5 1.5 pad_maximum_fusion.24
  (36 shorter events, 4.9 us)
Async XLA Ops:
  7.2 342.4 %reduce-scatter.7.cloned.1.call-start = ((), (), s32[]{:S(2)}) async-start(), calls=%async_computation.7 | async-start | bytes 5242880 | tf_op jit(solution)/shard_map/reduce_scatter | solution.py:75
  7.2 28.4 %copy-start.3 = (s32[2,1]{0,1:T(1,128)S(1)}, s32[2,1]{0,1:T(1,128)}, u32[]{:S(2)}) copy-start(s32[2,1]{0,1:T(1,128)} %param.7) | copy-start | bytes 28
  7.2 152.3 %collective-permute-start = (bf16[1024,1024]{1,0:T(8,128)(2,1)}, bf16[1024,1024]{1,0:T(8,128)(2,1)}, u32[]{:S(2)}, u32[]{:S(2)}) collective-permute-start(bf16[1024,1024]{1,0:T(8,128)(2,1)} %bitcast.82), channel_id=1, source_target_pairs={{0,2},{2,0},{1,3},{3,1},{4,6},{6,4},{5,7},{7,5},{8,10},{10,8},{9,1... | collective-permute-start | bytes 6291464 | tf_op jit(solution)/shard_map/ppermute | solution.py:27
  35.6 66.4 %collective-permute-start.4 = (bf16[1024,1024]{1,0:T(8,128)(2,1)}, bf16[1024,1024]{1,0:T(8,128)(2,1)}, u32[]{:S(2)}, u32[]{:S(2)}) collective-permute-start(bf16[1024,1024]{1,0:T(8,128)(2,1)} %add_convert_fusion.1), channel_id=1, source_target_pairs={{0,2},{2,0},{1,3},{3,1},{4,6},{6,4},{5,7},{7,5},{8,10},{10,8},{9,1... | collective-permute-start | bytes 6291464 | tf_op jit(solution)/shard_map/ppermute | solution.py:27
  37.5 109.4 %collective-permute-start.6 = (bf16[1024,1024]{1,0:T(8,128)(2,1)S(1)}, bf16[1024,1024]{1,0:T(8,128)(2,1)}, u32[]{:S(2)}, u32[]{:S(2)}) collective-permute-start(bf16[1024,1024]{1,0:T(8,128)(2,1)S(1)} %bitcast.74), channel_id=1, source_target_pairs={{0,2},{2,0},{1,3},{3,1},{4,6},{6,4},{5,7},{7,5},{8,10},{10,8},{9,1... | collective-permute-start | bytes 6291464 | tf_op jit(solution)/shard_map/ppermute | solution.py:27
  106.6 88.4 %collective-permute-start.5 = (bf16[2048,1024]{1,0:T(8,128)(2,1)}, bf16[2048,1024]{1,0:T(8,128)(2,1)}, u32[]{:S(2)}, u32[]{:S(2)}) collective-permute-start(bf16[2048,1024]{1,0:T(8,128)(2,1)} %pad_maximum_fusion.6), channel_id=1, source_target_pairs={{0,1},{1,0},{2,3},{3,2},{4,5},{5,4},{6,7},{7,6},{8,9},{9,8},{10,11... | collective-permute-start | bytes 12582920 | tf_op jit(solution)/shard_map/ppermute | solution.py:29
  132.0 59.1 %collective-permute-start.2 = (bf16[1024,1024]{1,0:T(8,128)(2,1)}, bf16[1024,1024]{1,0:T(8,128)(2,1)}, u32[]{:S(2)}, u32[]{:S(2)}) collective-permute-start(bf16[1024,1024]{1,0:T(8,128)(2,1)} %add_convert_fusion), channel_id=1, source_target_pairs={{0,2},{2,0},{1,3},{3,1},{4,6},{6,4},{5,7},{7,5},{8,10},{10,8},{9,1... | collective-permute-start | bytes 6291464 | tf_op jit(solution)/shard_map/ppermute | solution.py:27
  151.0 60.2 %collective-permute-start.7 = (bf16[2048,1024]{1,0:T(8,128)(2,1)}, bf16[2048,1024]{1,0:T(8,128)(2,1)}, u32[]{:S(2)}, u32[]{:S(2)}) collective-permute-start(bf16[2048,1024]{1,0:T(8,128)(2,1)} %pad_maximum_fusion.7), channel_id=1, source_target_pairs={{0,1},{1,0},{2,3},{3,2},{4,5},{5,4},{6,7},{7,6},{8,9},{9,8},{10,11... | collective-permute-start | bytes 12582920 | tf_op jit(solution)/shard_map/ppermute | solution.py:29
  151.0 8.6 %copy-start = (bf16[2,512,1024]{2,1,0:T(8,128)(2,1)S(1)}, bf16[2,512,1024]{2,1,0:T(8,128)(2,1)}, u32[]{:S(2)}) copy-start(bf16[2,512,1024]{2,1,0:T(8,128)(2,1)} %param.5) | copy-start | bytes 6291460
  155.1 35.9 %copy-start.2 = (bf16[1024,1024]{1,0:T(8,128)(2,1)S(1)}, bf16[1024,1024]{1,0:T(8,128)(2,1)}, u32[]{:S(2)}) copy-start(bf16[1024,1024]{1,0:T(8,128)(2,1)} %add_convert_fusion) | copy-start | bytes 6291460
  163.6 89.3 %collective-permute-start.1 = (bf16[2048,1024]{1,0:T(8,128)(2,1)}, bf16[2048,1024]{1,0:T(8,128)(2,1)}, u32[]{:S(2)}, u32[]{:S(2)}) collective-permute-start(bf16[2048,1024]{1,0:T(8,128)(2,1)} %pad_maximum_fusion.4), channel_id=1, source_target_pairs={{0,1},{1,0},{2,3},{3,2},{4,5},{5,4},{6,7},{7,6},{8,9},{9,8},{10,11... | collective-permute-start | bytes 12582920 | tf_op jit(solution)/shard_map/ppermute | solution.py:29
  195.0 73.9 %collective-permute-start.3 = (bf16[2048,1024]{1,0:T(8,128)(2,1)}, bf16[2048,1024]{1,0:T(8,128)(2,1)}, u32[]{:S(2)}, u32[]{:S(2)}) collective-permute-start(bf16[2048,1024]{1,0:T(8,128)(2,1)} %pad_maximum_fusion.5), channel_id=1, source_target_pairs={{0,1},{1,0},{2,3},{3,2},{4,5},{5,4},{6,7},{7,6},{8,9},{9,8},{10,11... | collective-permute-start | bytes 12582920 | tf_op jit(solution)/shard_map/ppermute | solution.py:29
  252.6 158.2 %reduce-scatter.5.cloned.1.call-start = ((), (), s32[]{:S(2)}) async-start(), calls=%async_computation.6 | async-start | bytes 5242880 | tf_op jit(solution)/shard_map/reduce_scatter | solution.py:75
  268.9 26.4 %copy-start.1 = (bf16[2,512,1024]{2,1,0:T(8,128)(2,1)S(1)}, bf16[2,512,1024]{2,1,0:T(8,128)(2,1)}, u32[]{:S(2)}) copy-start(bf16[2,512,1024]{2,1,0:T(8,128)(2,1)} %param.5) | copy-start | bytes 6291460
  310.2 180.2 %reduce-scatter.11.cloned.1.call-start = ((), (), s32[]{:S(2)}) async-start(), calls=%async_computation.9 | async-start | bytes 5242880 | tf_op jit(solution)/shard_map/reduce_scatter | solution.py:77
  329.6 240.3 %reduce-scatter.9.cloned.1.call-start = ((), (), s32[]{:S(2)}) async-start(), calls=%async_computation.8 | async-start | bytes 5242880 | tf_op jit(solution)/shard_map/reduce_scatter | solution.py:77
  349.6 61.2 %all-to-all-start.1 = ((f32[4,64,1024]{2,1,0:T(8,128)}), f32[4,64,1024]{2,1,0:T(8,128)S(1)}, u32[]{:S(2)}, u32[]{:S(2)}) async-start(f32[4,64,1024]{2,1,0:T(8,128)} %bitcast.87), calls=%async_computation.3 | async-start | bytes 2097152 | tf_op jit(solution)/shard_map/all_to_all | solution.py:79
  410.8 164.0 %all-to-all-start = ((f32[4,64,1024]{2,1,0:T(8,128)}), f32[4,64,1024]{2,1,0:T(8,128)S(1)}, u32[]{:S(2)}, u32[]{:S(2)}) async-start(f32[4,64,1024]{2,1,0:T(8,128)} %bitcast.88), calls=%async_computation.1 | async-start | bytes 2097152 | tf_op jit(solution)/shard_map/all_to_all | solution.py:79
Sparse Core Ops, SparseCore 0:
  252.7 78.4 reduce-scatter.6
  333.4 77.2 reduce-scatter.4
  413.1 77.2 reduce-scatter.10
  492.5 77.2 reduce-scatter.8
